TPU v7x, 32 devices: a whole 2x2x4 slice. The times are simulated.
32 devices in a mesh: rows: 8 (over z, x), cols: 4 (over y, core).
Axes of the slice: x: 2, y: 2, z: 4, core: 2. Of those that a mesh axis runs over, the one named last changes fastest.
Arguments:
- kernel_hat: bfloat16 [2, 256, 512, 1024], P(None, 'rows', 'cols'), may hold values from -0.5 to 0.5
- coefficients: float32 [128, 512], P(None, 'cols'), may hold values from -6 to 6
- wave_speed_sq: float32 [2048, 1024], P('rows', 'cols'), may hold values from 1 to 4
- wet_mask: int32 [2048, 1024], P('rows', 'cols'), may hold values 0 or 1
- boundary_cell: int32 [1024], replicated, may hold values from 0 to 1023, each once
- height: float32 [2048, 1024], P('rows', 'cols'), may hold values from -3 to 3
- flux_x: float32 [2048, 1024], P('rows', 'cols'), may hold values from -3 to 3
- flux_y: float32 [2048, 1024], P('rows', 'cols'), may hold values from -3 to 3
Outputs:
- boundary_series: float32 [128, 1024], P('rows', 'cols')
- height_out: float32 [2048, 1024], P('rows', 'cols')
- flux_x_out: float32 [2048, 1024], P('rows', 'cols')
- flux_y_out: float32 [2048, 1024], P('rows', 'cols')
Inputs may be any that keep to these rules, and one draw needn't show every extreme that they name: `boundary_cell`: each of the 1024 boundary points names a different grid column, so each column is named by exactly one point.
All inputs are finite; a program needn't handle non-finite values. No bound on the sum of `wet_mask` on one device may be relied on, other than what follows from the above.
Results may differ from a plain program's by a relative error of at most 0.0029.
Values sent between devices are 32-bit elements; how exact they have to be, the bound alone decides.
A program may use at most 64 MiB of HBM per device.

v0:
```python
import math

import jax
import jax.numpy as jnp
from jax import lax
from jax.sharding import PartitionSpec as P

STEP_RATIO = 0.25


def with_halo(cells, sides, width):
    for axis, dim in sides:
        count = lax.axis_size(axis)
        ends = count - 1
        head = lax.slice_in_dim(cells, 0, width, axis=dim)
        tail = lax.slice_in_dim(cells, cells.shape[dim] - width, cells.shape[dim], axis=dim)
        cells = jnp.concatenate(
            [
                lax.ppermute(tail, axis, [(i, (i + 1) % count) for i in range(ends)]),
                cells,
                lax.ppermute(head, axis, [((i + 1) % count, i) for i in range(ends)]),
            ],
            axis=dim,
        )
    return cells


def neighbours(values, along_dim):
    if along_dim == 1:
        return (values[1:-1, :-1], values[1:-1, 1:])
    return (values[:-1, 1:-1], values[1:, 1:-1])


def face_fluxes(surface, along, across, speed_sq, celerity, wet, along_dim):
    left_surf, right_surf = neighbours(surface, along_dim)
    left_along, right_along = neighbours(along, along_dim)
    left_across, right_across = neighbours(across, along_dim)
    left_sq, right_sq = neighbours(speed_sq, along_dim)
    left_speed, right_speed = neighbours(celerity, along_dim)
    left_wet, right_wet = neighbours(wet, along_dim)
    opened = left_wet * right_wet
    damping = 0.25 * (left_speed + right_speed)
    mass_flux = opened * (0.5 * (left_along + right_along) - damping * (right_surf - left_surf))
    momentum = opened * (
        0.5 * (left_sq * left_surf + right_sq * right_surf) - damping * (right_along - left_along)
    )
    shear_flux = opened * (-damping * (right_across - left_across))
    return (mass_flux, momentum, shear_flux)


def advance(surface, along_x, along_y, speed_sq, wet):
    celerity = jnp.sqrt(speed_sq)
    mass_x, momentum_x, shear_x = face_fluxes(surface, along_x, along_y, speed_sq, celerity, wet, 1)
    mass_y, momentum_y, shear_y = face_fluxes(surface, along_y, along_x, speed_sq, celerity, wet, 0)
    interior_wet = wet[1:-1, 1:-1]

    def update(values, flux_cols, flux_rows):
        change = flux_cols[:, 1:] - flux_cols[:, :-1] + (flux_rows[1:] - flux_rows[:-1])
        return interior_wet * (values[1:-1, 1:-1] - STEP_RATIO * change)

    return (
        update(surface, mass_x, mass_y),
        update(along_x, momentum_x, shear_y),
        update(along_y, shear_x, momentum_y),
    )


def set_row(values, position, replacement, flag):
    return values.at[position].set(jnp.where(flag, replacement, values[position]))


def on_device(
    kernel_hat, coefficients, wave_speed_sq, wet_mask, boundary_cell, height, flux_x, flux_y
):
    high = lax.Precision.HIGHEST
    freq_dev = kernel_hat.shape[1]
    steps_total = coefficients.shape[0]
    freq_total = freq_dev * lax.axis_size("rows")
    freqs = lax.axis_index("rows") * freq_dev + jnp.arange(freq_dev, dtype=jnp.int32)
    times = jnp.arange(steps_total, dtype=jnp.int32)
    factor = 2.0 * math.pi / freq_total
    forward = (freqs[:, None] * times[None, :] % freq_total).astype(jnp.float32) * factor
    coef_re = jnp.dot(jnp.cos(forward), coefficients, precision=high).astype(jnp.bfloat16)
    coef_im = (-jnp.dot(jnp.sin(forward), coefficients, precision=high)).astype(jnp.bfloat16)
    form = "fso,fs->fo"
    kern_re = kernel_hat[0]
    kern_im = kernel_hat[1]
    spec_re = jnp.einsum(form, kern_re, coef_re, preferred_element_type=jnp.float32) - jnp.einsum(
        form, kern_im, coef_im, preferred_element_type=jnp.float32
    )
    spec_im = jnp.einsum(form, kern_re, coef_im, preferred_element_type=jnp.float32) + jnp.einsum(
        form, kern_im, coef_re, preferred_element_type=jnp.float32
    )
    inverse = (times[:, None] * freqs[None, :] % freq_total).astype(jnp.float32) * factor
    inv_cos = jnp.cos(inverse) / freq_total
    inv_sin = jnp.sin(inverse) / freq_total
    whole = jnp.dot(inv_cos, spec_re, precision=high) - jnp.dot(inv_sin, spec_im, precision=high)
    partial_value = lax.psum_scatter(whole, "cols", scatter_dimension=1, tiled=True)
    series = lax.psum_scatter(partial_value, "rows", scatter_dimension=0, tiled=True)
    latest = lax.all_gather(series[-2:], "cols", axis=1, tiled=True)
    tile_width = height.shape[1]
    columns = lax.axis_index("cols") * tile_width - 2 + jnp.arange(tile_width + 4, dtype=jnp.int32)
    selector = (boundary_cell[:, None] == columns[None, :]).astype(jnp.float32)
    ghost_wide = jnp.dot(latest, selector, precision=high)
    at_edge = lax.axis_index("rows") == lax.axis_size("rows") - 1
    wet = wet_mask.astype(jnp.float32)
    speed_pad, wet_pad = (
        with_halo(wave_speed_sq, (("rows", 0), ("cols", 1)), 2),
        with_halo(wet, (("rows", 0), ("cols", 1)), 2),
    )
    speed_pad = set_row(speed_pad, -2, 1.0, at_edge)
    wet_pad = set_row(wet_pad, -2, 1.0, at_edge)
    surf_pad, pad_x, pad_y = (
        with_halo(height, (("rows", 0), ("cols", 1)), 2),
        with_halo(flux_x, (("rows", 0), ("cols", 1)), 2),
        with_halo(flux_y, (("rows", 0), ("cols", 1)), 2),
    )
    surf_pad = set_row(surf_pad, -2, ghost_wide[0], at_edge)
    surface, along_x, along_y = advance(surf_pad, pad_x, pad_y, speed_pad, wet_pad)
    surface = set_row(surface, -1, ghost_wide[1, 1:-1], at_edge)
    along_x = set_row(along_x, -1, 0.0, at_edge)
    along_y = set_row(along_y, -1, 0.0, at_edge)
    surface, along_x, along_y = advance(
        surface, along_x, along_y, speed_pad[1:-1, 1:-1], wet_pad[1:-1, 1:-1]
    )
    return (series, surface, along_x, along_y)


def solution(mesh):
    return jax.shard_map(
        on_device,
        mesh=mesh,
        in_specs=(
            P(None, "rows", "cols", None),
            P(None, "cols"),
            P("rows", "cols"),
            P("rows", "cols"),
            P(),
            P("rows", "cols"),
            P("rows", "cols"),
            P("rows", "cols"),
        ),
        out_specs=(P("rows", "cols"), P("rows", "cols"), P("rows", "cols"), P("rows", "cols")),
        check_vma=False,
    )
```

profile of v0, /device:TPU:0, one launch (start us, length us, event | category | flops | bytes accessed | tf_op | source)
XLA Modules:
  0.0 183.8 jit_solution(7591247571799552067)
XLA Ops:
  8.2 4.9 %collective-permute-start = (f32[2,256]{1,0:T(2,128)S(1)}, f32[2,256]{1,0:T(2,128)S(1)}, u32[]{:S(2)}, u32[]{:S(2)}) collective-permute-start(f32[2,256]{1,0:T(2,128)S(1)} %get-tuple-element.104), channel_id=1, source_target_pairs={{0,4},{4,8},{8,12},{12,16},{16,20},{20,24},{24,28},{1,5},{5,9},{9,... | collective-permute-start | bytes 6152 | tf_op jit(solution)/shard_map/ppermute | solution.py:19
  13.1 1.3 collective-permute-start.1
  15.0 4.7 %fusion.6 = f32[32,1,1024]{2,1,0:T(1,128)S(1)} fusion(bf16[2,32,128,1024]{3,2,1,0:T(8,128)(2,1)} %param.20, bf16[32,128,1]{1,0,2:T(8,128)(2,1)S(1)} %fusion.15), kind=kOutput, calls=%fused_computation.6 | convolution fusion | flops 8388608 | bytes 8527872 | tf_op jit(solution)/shard_map/fso,fs->fo/dot_general | solution.py:88
  19.8 5.3 %fusion = f32[32,1,1024]{2,1,0:T(1,128)S(1)} fusion(bf16[2,32,128,1024]{3,2,1,0:T(8,128)(2,1)} %param.20, bf16[32,128,1]{1,0,2:T(8,128)(2,1)S(1)} %fusion.15), kind=kOutput, calls=%fused_computation | convolution fusion | flops 8388608 | bytes 8527872 | tf_op jit(solution)/shard_map/fso,fs->fo/dot_general | solution.py:91
  28.8 1.7 convolution_subtract_fusion
  30.6 4.5 %collective-permute-start.4 = (f32[2,256]{1,0:T(2,128)S(1)}, f32[2,256]{1,0:T(2,128)S(1)}, u32[]{:S(2)}, u32[]{:S(2)}) collective-permute-start(f32[2,256]{1,0:T(2,128)S(1)} %get-tuple-element.108), channel_id=1, source_target_pairs={{0,4},{4,8},{8,12},{12,16},{16,20},{20,24},{24,28},{1,5},{5,9},{9,... | collective-permute-start | bytes 6152 | tf_op jit(solution)/shard_map/ppermute | solution.py:19
  35.1 1.3 collective-permute-start.5
  36.4 5.0 %collective-permute-start.12 = (f32[2,256]{1,0:T(2,128)S(1)}, f32[2,256]{1,0:T(2,128)S(1)}, u32[]{:S(2)}, u32[]{:S(2)}) collective-permute-start(f32[2,256]{1,0:T(2,128)S(1)} %get-tuple-element.102), channel_id=1, source_target_pairs={{0,4},{4,8},{8,12},{12,16},{16,20},{20,24},{24,28},{1,5},{5,9},{9,... | collective-permute-start | bytes 6152 | tf_op jit(solution)/shard_map/ppermute | solution.py:19
  42.8 5.4 %collective-permute-start.16 = (f32[2,256]{1,0:T(2,128)S(1)}, f32[2,256]{1,0:T(2,128)S(1)}, u32[]{:S(2)}, u32[]{:S(2)}) collective-permute-start(f32[2,256]{1,0:T(2,128)S(1)} %get-tuple-element.106), channel_id=1, source_target_pairs={{0,4},{4,8},{8,12},{12,16},{16,20},{20,24},{24,28},{1,5},{5,9},{9,... | collective-permute-start | bytes 6152 | tf_op jit(solution)/shard_map/ppermute | solution.py:19
  49.7 5.4 %collective-permute-start.8 = (f32[2,256]{1,0:T(2,128)S(1)}, f32[2,256]{1,0:T(2,128)S(1)}, u32[]{:S(2)}, u32[]{:S(2)}) collective-permute-start(f32[2,256]{1,0:T(2,128)S(1)} %get-tuple-element.100), channel_id=1, source_target_pairs={{0,4},{4,8},{8,12},{12,16},{16,20},{20,24},{24,28},{1,5},{5,9},{9,... | collective-permute-start | bytes 6152 | tf_op jit(solution)/shard_map/ppermute | solution.py:19
  55.3 1.3 collective-permute-start.9
  56.7 1.3 collective-permute-start.2
  59.4 4.8 %collective-permute-start.6 = (f32[260,2]{1,0:T(8,128)S(1)}, f32[260,2]{1,0:T(8,128)S(1)}, u32[]{:S(2)}, u32[]{:S(2)}) collective-permute-start(f32[260,2]{1,0:T(8,128)S(1)} %get-tuple-element.98), channel_id=1, source_target_pairs={{0,1},{1,2},{2,3},{4,5},{5,6},{6,7},{8,9},{9,10},{10,11},{12,13},{... | collective-permute-start | bytes 6248 | tf_op jit(solution)/shard_map/ppermute | solution.py:19
  65.7 4.3 %collective-permute-start.14 = (f32[260,2]{1,0:T(8,128)S(1)}, f32[260,2]{1,0:T(8,128)S(1)}, u32[]{:S(2)}, u32[]{:S(2)}) collective-permute-start(f32[260,2]{1,0:T(8,128)S(1)} %get-tuple-element.92), channel_id=1, source_target_pairs={{0,1},{1,2},{2,3},{4,5},{5,6},{6,7},{8,9},{9,10},{10,11},{12,13},{... | collective-permute-start | bytes 6248 | tf_op jit(solution)/shard_map/ppermute | solution.py:19
  72.0 4.3 %collective-permute-start.18 = (f32[260,2]{1,0:T(8,128)S(1)}, f32[260,2]{1,0:T(8,128)S(1)}, u32[]{:S(2)}, u32[]{:S(2)}) collective-permute-start(f32[260,2]{1,0:T(8,128)S(1)} %get-tuple-element.96), channel_id=1, source_target_pairs={{0,1},{1,2},{2,3},{4,5},{5,6},{6,7},{8,9},{9,10},{10,11},{12,13},{... | collective-permute-start | bytes 6248 | tf_op jit(solution)/shard_map/ppermute | solution.py:19
  77.9 4.3 %collective-permute-start.10 = (f32[260,2]{1,0:T(8,128)}, f32[260,2]{1,0:T(8,128)S(1)}, u32[]{:S(2)}, u32[]{:S(2)}) collective-permute-start(f32[260,2]{1,0:T(8,128)} %get-tuple-element.90), channel_id=1, source_target_pairs={{0,1},{1,2},{2,3},{4,5},{5,6},{6,7},{8,9},{9,10},{10,11},{12,13},{... | collective-permute-start | bytes 6248 | tf_op jit(solution)/shard_map/ppermute | solution.py:19
  84.4 2.5 %collective-permute-done.11 = f32[260,2]{1,0:T(8,128)S(1)} collective-permute-done((f32[260,2]{1,0:T(8,128)S(1)}, f32[260,2]{1,0:T(8,128)S(1)}, u32[]{:S(2)}, u32[]{:S(2)}) %collective-permute-start.11) | collective-permute-done | bytes 2112 | tf_op jit(solution)/shard_map/ppermute | solution.py:21
  88.5 1.4 fusion.34
  89.9 66.6 %reduce-scatter.5.cloned.1.call-done = f32[16,256]{1,0:T(8,128)} async-done(((f32[128,256]{1,0:T(8,128)}), f32[16,256]{1,0:T(8,128)}) %reduce-scatter.5.cloned.1.call-update) | async-done | bytes 16400 | tf_op jit(solution)/shard_map/reduce_scatter | solution.py:99
  157.2 5.2 %all_gather.3 = f32[2,1024]{1,0:T(2,128)S(1)} all-gather(f32[2,256]{1,0:T(2,128)S(1)} %slice.557), channel_id=1, replica_groups=mesh['rows'=8,'cols'=4] {'cols'}, dimensions={1}, use_global_device_ids=true | all-gather | bytes 10240 | tf_op jit(solution)/shard_map/all_gather | solution.py:100
  166.9 1.3 scatter.26
  168.2 1.7 fusion.57
  169.9 2.9 %fusion.50 = (f32[256,257]{1,0:T(8,128)}, f32[256,257]{1,0:T(8,128)}) fusion(f32[260,260]{1,0:T(8,128)S(1)} %scatter.24, f32[258,258]{1,0:T(8,128)S(1)} %scatter.25, f32[258,258]{1,0:T(8,128)} %scatter.26, f32[260,260]{1,0:T(8,128)S(1)} %scatter.20, f32[258,258]{1,0:T(8,128)S(1)} %slice_sqrt_fusion), kind=kLoop, calls=%fused_computation.79 | loop fusion | flops 1118464 | bytes 3158016 | tf_op jit(solution)/shard_map/mul | solution.py:44
  174.2 2.8 %fusion.62 = (f32[256,256]{1,0:T(8,128)}, f32[256,256]{1,0:T(8,128)}, f32[256,256]{1,0:T(8,128)}) fusion(f32[257,256]{1,0:T(8,128)S(1)} %get-tuple-element.76, f32[256,257]{1,0:T(8,128)S(1)} %fusion.46, f32[258,258]{1,0:T(8,128)S(1)} %scatter.29, f32[260,260]{1,0:T(8,128)S(1)} %scatter.20, f32[257,256]{1,0:T(8,128)S(1)} %fusion.57, ...), kind=kLoop, calls=%fused_computation.107 | loop fusion | flops 1179648 | bytes 4980736 | tf_op jit(solution)/shard_map/mul | solution.py:59
  (101 shorter events, 24.9 us)
Async XLA Ops:
  7.2 81.3 %reduce-scatter.3.cloned.1.call-start = ((), (), s32[]{:S(2)}) async-start(), calls=%async_computation.2 | async-start | bytes 655360 | tf_op jit(solution)/shard_map/reduce_scatter | solution.py:98
  8.2 33.3 %collective-permute-start = (f32[2,256]{1,0:T(2,128)S(1)}, f32[2,256]{1,0:T(2,128)S(1)}, u32[]{:S(2)}, u32[]{:S(2)}) collective-permute-start(f32[2,256]{1,0:T(2,128)S(1)} %get-tuple-element.104), channel_id=1, source_target_pairs={{0,4},{4,8},{8,12},{12,16},{16,20},{20,24},{24,28},{1,5},{5,9},{9,... | collective-permute-start | bytes 6152 | tf_op jit(solution)/shard_map/ppermute | solution.py:19
  13.1 29.7 %collective-permute-start.1 = (f32[2,256]{1,0:T(2,128)S(1)}, f32[2,256]{1,0:T(2,128)S(1)}, u32[]{:S(2)}, u32[]{:S(2)}) collective-permute-start(f32[2,256]{1,0:T(2,128)S(1)} %get-tuple-element.105), channel_id=1, source_target_pairs={{4,0},{8,4},{12,8},{16,12},{20,16},{24,20},{28,24},{5,1},{9,5},{13... | collective-permute-start | bytes 6152 | tf_op jit(solution)/shard_map/ppermute | solution.py:21
  25.6 15.9 %copy-start.9 = (f32[256,256]{1,0:T(8,128)S(1)}, f32[256,256]{1,0:T(8,128)}, u32[]{:S(2)}) copy-start(f32[256,256]{1,0:T(8,128)} %param.26) | copy-start | bytes 786436
  30.5 126.0 %reduce-scatter.5.cloned.1.call-start = ((), (), s32[]{:S(2)}) async-start(), calls=%async_computation.3 | async-start | bytes 147456 | tf_op jit(solution)/shard_map/reduce_scatter | solution.py:99
  30.6 17.9 %collective-permute-start.4 = (f32[2,256]{1,0:T(2,128)S(1)}, f32[2,256]{1,0:T(2,128)S(1)}, u32[]{:S(2)}, u32[]{:S(2)}) collective-permute-start(f32[2,256]{1,0:T(2,128)S(1)} %get-tuple-element.108), channel_id=1, source_target_pairs={{0,4},{4,8},{8,12},{12,16},{16,20},{20,24},{24,28},{1,5},{5,9},{9,... | collective-permute-start | bytes 6152 | tf_op jit(solution)/shard_map/ppermute | solution.py:19
  35.1 14.6 %collective-permute-start.5 = (f32[2,256]{1,0:T(2,128)S(1)}, f32[2,256]{1,0:T(2,128)S(1)}, u32[]{:S(2)}, u32[]{:S(2)}) collective-permute-start(f32[2,256]{1,0:T(2,128)S(1)} %get-tuple-element.109), channel_id=1, source_target_pairs={{4,0},{8,4},{12,8},{16,12},{20,16},{24,20},{28,24},{5,1},{9,5},{13... | collective-permute-start | bytes 6152 | tf_op jit(solution)/shard_map/ppermute | solution.py:21
  36.4 18.9 %collective-permute-start.12 = (f32[2,256]{1,0:T(2,128)S(1)}, f32[2,256]{1,0:T(2,128)S(1)}, u32[]{:S(2)}, u32[]{:S(2)}) collective-permute-start(f32[2,256]{1,0:T(2,128)S(1)} %get-tuple-element.102), channel_id=1, source_target_pairs={{0,4},{4,8},{8,12},{12,16},{16,20},{20,24},{24,28},{1,5},{5,9},{9,... | collective-permute-start | bytes 6152 | tf_op jit(solution)/shard_map/ppermute | solution.py:19
  41.5 15.1 %collective-permute-start.13 = (f32[2,256]{1,0:T(2,128)S(1)}, f32[2,256]{1,0:T(2,128)S(1)}, u32[]{:S(2)}, u32[]{:S(2)}) collective-permute-start(f32[2,256]{1,0:T(2,128)S(1)} %get-tuple-element.103), channel_id=1, source_target_pairs={{4,0},{8,4},{12,8},{16,12},{20,16},{24,20},{28,24},{5,1},{9,5},{13... | collective-permute-start | bytes 6152 | tf_op jit(solution)/shard_map/ppermute | solution.py:21
  42.8 15.3 %collective-permute-start.16 = (f32[2,256]{1,0:T(2,128)S(1)}, f32[2,256]{1,0:T(2,128)S(1)}, u32[]{:S(2)}, u32[]{:S(2)}) collective-permute-start(f32[2,256]{1,0:T(2,128)S(1)} %get-tuple-element.106), channel_id=1, source_target_pairs={{0,4},{4,8},{8,12},{12,16},{16,20},{20,24},{24,28},{1,5},{5,9},{9,... | collective-permute-start | bytes 6152 | tf_op jit(solution)/shard_map/ppermute | solution.py:19
  48.4 114.0 %copy-start.10 = (s32[1024]{0:T(1024)S(1)}, s32[1024]{0:T(1024)}, u32[]{:S(2)}) copy-start(s32[1024]{0:T(1024)} %param.24) | copy-start | bytes 12292
  48.4 11.0 %collective-permute-start.17 = (f32[2,256]{1,0:T(2,128)S(1)}, f32[2,256]{1,0:T(2,128)S(1)}, u32[]{:S(2)}, u32[]{:S(2)}) collective-permute-start(f32[2,256]{1,0:T(2,128)S(1)} %get-tuple-element.107), channel_id=1, source_target_pairs={{4,0},{8,4},{12,8},{16,12},{20,16},{24,20},{28,24},{5,1},{9,5},{13... | collective-permute-start | bytes 6152 | tf_op jit(solution)/shard_map/ppermute | solution.py:21
  49.7 14.6 %collective-permute-start.8 = (f32[2,256]{1,0:T(2,128)S(1)}, f32[2,256]{1,0:T(2,128)S(1)}, u32[]{:S(2)}, u32[]{:S(2)}) collective-permute-start(f32[2,256]{1,0:T(2,128)S(1)} %get-tuple-element.100), channel_id=1, source_target_pairs={{0,4},{4,8},{8,12},{12,16},{16,20},{20,24},{24,28},{1,5},{5,9},{9,... | collective-permute-start | bytes 6152 | tf_op jit(solution)/shard_map/ppermute | solution.py:19
  55.3 10.3 %collective-permute-start.9 = (f32[2,256]{1,0:T(2,128)S(1)}, f32[2,256]{1,0:T(2,128)S(1)}, u32[]{:S(2)}, u32[]{:S(2)}) collective-permute-start(f32[2,256]{1,0:T(2,128)S(1)} %get-tuple-element.101), channel_id=1, source_target_pairs={{4,0},{8,4},{12,8},{16,12},{20,16},{24,20},{28,24},{5,1},{9,5},{13... | collective-permute-start | bytes 6152 | tf_op jit(solution)/shard_map/ppermute | solution.py:21
  56.7 14.1 %collective-permute-start.2 = (f32[260,2]{1,0:T(8,128)S(1)}, f32[260,2]{1,0:T(8,128)S(1)}, u32[]{:S(2)}, u32[]{:S(2)}) collective-permute-start(f32[260,2]{1,0:T(8,128)S(1)} %get-tuple-element.94), channel_id=1, source_target_pairs={{0,1},{1,2},{2,3},{4,5},{5,6},{6,7},{8,9},{9,10},{10,11},{12,13},{... | collective-permute-start | bytes 6248 | tf_op jit(solution)/shard_map/ppermute | solution.py:19
  58.1 13.9 %collective-permute-start.3 = (f32[260,2]{1,0:T(8,128)S(1)}, f32[260,2]{1,0:T(8,128)S(1)}, u32[]{:S(2)}, u32[]{:S(2)}) collective-permute-start(f32[260,2]{1,0:T(8,128)S(1)} %get-tuple-element.95), channel_id=1, source_target_pairs={{1,0},{2,1},{3,2},{5,4},{6,5},{7,6},{9,8},{10,9},{11,10},{13,12},{... | collective-permute-start | bytes 6248 | tf_op jit(solution)/shard_map/ppermute | solution.py:21
  59.4 23.0 %collective-permute-start.6 = (f32[260,2]{1,0:T(8,128)S(1)}, f32[260,2]{1,0:T(8,128)S(1)}, u32[]{:S(2)}, u32[]{:S(2)}) collective-permute-start(f32[260,2]{1,0:T(8,128)S(1)} %get-tuple-element.98), channel_id=1, source_target_pairs={{0,1},{1,2},{2,3},{4,5},{5,6},{6,7},{8,9},{9,10},{10,11},{12,13},{... | collective-permute-start | bytes 6248 | tf_op jit(solution)/shard_map/ppermute | solution.py:19
  64.4 19.3 %collective-permute-start.7 = (f32[260,2]{1,0:T(8,128)S(1)}, f32[260,2]{1,0:T(8,128)S(1)}, u32[]{:S(2)}, u32[]{:S(2)}) collective-permute-start(f32[260,2]{1,0:T(8,128)S(1)} %get-tuple-element.99), channel_id=1, source_target_pairs={{1,0},{2,1},{3,2},{5,4},{6,5},{7,6},{9,8},{10,9},{11,10},{13,12},{... | collective-permute-start | bytes 6248 | tf_op jit(solution)/shard_map/ppermute | solution.py:21
  65.7 10.9 %collective-permute-start.14 = (f32[260,2]{1,0:T(8,128)S(1)}, f32[260,2]{1,0:T(8,128)S(1)}, u32[]{:S(2)}, u32[]{:S(2)}) collective-permute-start(f32[260,2]{1,0:T(8,128)S(1)} %get-tuple-element.92), channel_id=1, source_target_pairs={{0,1},{1,2},{2,3},{4,5},{5,6},{6,7},{8,9},{9,10},{10,11},{12,13},{... | collective-permute-start | bytes 6248 | tf_op jit(solution)/shard_map/ppermute | solution.py:19
  70.7 7.1 %collective-permute-start.15 = (f32[260,2]{1,0:T(8,128)S(1)}, f32[260,2]{1,0:T(8,128)S(1)}, u32[]{:S(2)}, u32[]{:S(2)}) collective-permute-start(f32[260,2]{1,0:T(8,128)S(1)} %get-tuple-element.93), channel_id=1, source_target_pairs={{1,0},{2,1},{3,2},{5,4},{6,5},{7,6},{9,8},{10,9},{11,10},{13,12},{... | collective-permute-start | bytes 6248 | tf_op jit(solution)/shard_map/ppermute | solution.py:21
  72.0 11.9 %collective-permute-start.18 = (f32[260,2]{1,0:T(8,128)S(1)}, f32[260,2]{1,0:T(8,128)S(1)}, u32[]{:S(2)}, u32[]{:S(2)}) collective-permute-start(f32[260,2]{1,0:T(8,128)S(1)} %get-tuple-element.96), channel_id=1, source_target_pairs={{0,1},{1,2},{2,3},{4,5},{5,6},{6,7},{8,9},{9,10},{10,11},{12,13},{... | collective-permute-start | bytes 6248 | tf_op jit(solution)/shard_map/ppermute | solution.py:19
  76.6 7.4 %collective-permute-start.19 = (f32[260,2]{1,0:T(8,128)S(1)}, f32[260,2]{1,0:T(8,128)S(1)}, u32[]{:S(2)}, u32[]{:S(2)}) collective-permute-start(f32[260,2]{1,0:T(8,128)S(1)} %get-tuple-element.97), channel_id=1, source_target_pairs={{1,0},{2,1},{3,2},{5,4},{6,5},{7,6},{9,8},{10,9},{11,10},{13,12},{... | collective-permute-start | bytes 6248 | tf_op jit(solution)/shard_map/ppermute | solution.py:21
  77.9 6.5 %collective-permute-start.10 = (f32[260,2]{1,0:T(8,128)}, f32[260,2]{1,0:T(8,128)S(1)}, u32[]{:S(2)}, u32[]{:S(2)}) collective-permute-start(f32[260,2]{1,0:T(8,128)} %get-tuple-element.90), channel_id=1, source_target_pairs={{0,1},{1,2},{2,3},{4,5},{5,6},{6,7},{8,9},{9,10},{10,11},{12,13},{... | collective-permute-start | bytes 6248 | tf_op jit(solution)/shard_map/ppermute | solution.py:19
  82.4 4.5 %collective-permute-start.11 = (f32[260,2]{1,0:T(8,128)S(1)}, f32[260,2]{1,0:T(8,128)S(1)}, u32[]{:S(2)}, u32[]{:S(2)}) collective-permute-start(f32[260,2]{1,0:T(8,128)S(1)} %get-tuple-element.91), channel_id=1, source_target_pairs={{1,0},{2,1},{3,2},{5,4},{6,5},{7,6},{9,8},{10,9},{11,10},{13,12},{... | collective-permute-start | bytes 6248 | tf_op jit(solution)/shard_map/ppermute | solution.py:21
  (9 other events, 60.0 us)
Sparse Core Ops, SparseCore 0:
  30.6 24.0 reduce-scatter.2
  88.6 67.8 reduce-scatter.4
where the time goes:
time: 185 us; the launch traced here: 184 us
  waiting for transfers between devices  69.1 us (37%)
  starting transfers between devices  57.2 us (31%)
  other arithmetic  16.3 us (9%)
  matrix products  16.1 us (9%)
  between operations  14.8 us (8%)
  blocking collectives  5.18 us (3%)
  local copies, waits for them, and re-layouts  5.03 us (3%)
    reduce_scatter x1, waiting for transfers between devices, on_device(): lax.psum_scatter(partial_value, 'rows', scatter_dimension=0, tiled=True)  66.6 us
    ppermute x10, starting transfers between devices, with_halo(): lax.ppermute(tail, axis, [(i, (i + 1) % count) for i in range(ends)])  44.2 us
    ppermute x10, starting transfers between devices, with_halo(): lax.ppermute(head, axis, [((i + 1) % count, i) for i in range(ends)])  12.9 us
    mul x4, other arithmetic, face_fluxes(): opened * (0.5 * (left_sq * left_surf + right_sq * right_surf) - damping *...  5.57 us
    dot_general x1, matrix products, on_device(): jnp.einsum(form, kern_im, coef_re, preferred_element_type=jnp.float32)  5.33 us
    all_gather x1, blocking collectives, on_device(): latest = lax.all_gather(series[-2:], 'cols', axis=1, tiled=True)  5.18 us
    mul x4, other arithmetic, face_fluxes(): shear_flux = opened * (-damping * (right_across - left_across))  4.81 us
    dot_general x1, matrix products, on_device(): jnp.einsum(form, kern_re, coef_re, preferred_element_type=jnp.float32)  4.72 us
  transfers between devices with their start and end apart: 22, of which 2 were waited for; matrix products, arithmetic and copies ran while one was open for 11% of the time, Pallas kernels for 0%

commit v1 on v0

v1 whole, which is shorter than its diff:
```python
import functools
import math

import jax
import jax.numpy as jnp
import numpy as np
from jax import lax
from jax.experimental import pallas as pl
from jax.experimental.pallas import tpu as pltpu
from jax.sharding import PartitionSpec as P

MESH = pl.DeviceIdType.MESH
GROUP = 8
EDGE = 8
LANE = 128
F32 = jnp.float32
BF16 = jnp.bfloat16


def tables(freq_total, steps, row_devs):
    freq = np.arange(freq_total)
    time = np.arange(steps)
    phase = 2.0 * math.pi * (np.outer(freq, time) % freq_total) / freq_total
    cos = np.cos(phase).reshape(row_devs, -1, GROUP, steps)
    sin = np.sin(phase).reshape(row_devs, -1, GROUP, steps)
    both = np.concatenate([cos, -sin], axis=2).reshape(row_devs, -1, steps)
    forward = both.astype(np.float32)
    inverse = np.swapaxes(both, 1, 2) / freq_total
    high = inverse.astype(np.float32).astype(jnp.bfloat16)
    low = (inverse - high.astype(np.float64)).astype(np.float32).astype(jnp.bfloat16)
    return forward, np.concatenate([high, high, low], axis=2)


def split(value):
    high = value.astype(BF16)
    return high, value - high.astype(F32)


def faces(speed, wet, dim):
    ahead = speed.shape[dim] - 1
    opened = wet * pltpu.roll(wet, ahead, dim)
    return 0.5 * opened, opened * (0.25 * (speed + pltpu.roll(speed, ahead, dim)))


def step_once(surf, qx, qy, speed_sq, wet, face_x, face_y):
    energy = speed_sq * surf
    change = []
    for dim, along, across, (half, damp) in ((1, qx, qy, face_x), (0, qy, qx, face_y)):
        ahead = surf.shape[dim] - 1
        later = lambda v: pltpu.roll(v, ahead, dim)
        mass = half * (along + later(along)) - damp * (later(surf) - surf)
        momentum = half * (energy + later(energy)) - damp * (later(along) - along)
        shear = -damp * (later(across) - across)
        change.append([f - pltpu.roll(f, 1, dim) for f in (mass, momentum, shear)])
    (mass_x, mom_x, shear_x), (mass_y, mom_y, shear_y) = change
    return (
        wet * (surf - 0.25 * (mass_x + mass_y)),
        wet * (qx - 0.25 * (mom_x + shear_y)),
        wet * (qy - 0.25 * (shear_x + mom_y)),
    )


def kernel(
    n_rows, n_cols,
    kern_hbm, coef_hbm, sq_hbm, wet_hbm, cell_hbm, surf_hbm, qx_hbm, qy_hbm, fwd_hbm, inv_hbm,
    series_hbm, surf_out, qx_out, qy_out,
    kern, coef, fwd, inv, cells, pad, wet_int, wet_pad, corner, corner_wet,
    strip_out, strip_in, spec_out, spec_in, whole_buf, whole_in, series_buf, late_in,
    mid, out_buf,
    local_sem, kern_sem, halo_send, halo_recv, spec_send, spec_recv,
    whole_send, whole_recv, late_send, late_recv, out_sem,
):
    row = lax.axis_index("rows")
    col = lax.axis_index("cols")
    freqs, src, obs = kern.shape[1:]
    groups = freqs // GROUP
    tall, wide = surf_hbm.shape
    points = obs // n_cols
    own_steps = series_buf.shape[0]
    has_n, has_s = row > 0, row < n_rows - 1
    has_w, has_e = col > 0, col < n_cols - 1
    at_edge = row == n_rows - 1

    inputs = [
        pltpu.make_async_copy(coef_hbm, coef, local_sem.at[0]),
        pltpu.make_async_copy(fwd_hbm.at[row], fwd, local_sem.at[1]),
        pltpu.make_async_copy(surf_hbm, pad.at[0, :tall, :wide], local_sem.at[2]),
        pltpu.make_async_copy(qx_hbm, pad.at[1, :tall, :wide], local_sem.at[3]),
        pltpu.make_async_copy(qy_hbm, pad.at[2, :tall, :wide], local_sem.at[4]),
        pltpu.make_async_copy(sq_hbm, pad.at[3, :tall, :wide], local_sem.at[5]),
        pltpu.make_async_copy(wet_hbm, wet_int.at[:tall], local_sem.at[6]),
        pltpu.make_async_copy(inv_hbm.at[row], inv, local_sem.at[7]),
        pltpu.make_async_copy(cell_hbm, cells, local_sem.at[8]),
    ]
    for copy in inputs:
        copy.start()
    chunks = []
    for g in range(groups):
        for part in range(2):
            where = pl.ds(g * GROUP, GROUP)
            copy = pltpu.make_async_copy(
                kern_hbm.at[part, where], kern.at[part, where], kern_sem.at[g, part]
            )
            copy.start()
            chunks.append(copy)

    diagonals = [
        (has_n & has_w, -1, -1), (has_n & has_e, -1, 1),
        (has_s & has_w, 1, -1), (has_s & has_e, 1, 1),
    ]
    barrier = pltpu.get_barrier_semaphore()
    for k in range(1, n_rows):
        pl.semaphore_signal(barrier, 1, device_id=(lax.rem(row + k, n_rows), col), device_id_type=MESH)
    for k in range(1, n_cols):
        pl.semaphore_signal(barrier, 1, device_id=(row, lax.rem(col + k, n_cols)), device_id_type=MESH)
    for exists, dr, dc in diagonals:
        @pl.when(exists)
        def _(dr=dr, dc=dc):
            pl.semaphore_signal(barrier, 1, device_id=(row + dr, col + dc), device_id_type=MESH)

    inputs[0].wait()
    inputs[1].wait()
    spectrum = jnp.dot(
        fwd[...], coef[...], precision=lax.Precision.HIGHEST, preferred_element_type=F32
    )

    for copy in inputs[2:7]:
        copy.wait()
    lane = lax.broadcasted_iota(jnp.int32, (tall, LANE), 1)
    packed = jnp.zeros((tall, LANE), F32)
    for k in range(5):
        if k < 4:
            first, last = pad[k, :tall, :LANE], pad[k, :tall, wide - LANE:wide]
        else:
            first = wet_int[:tall, :LANE].astype(F32)
            last = wet_int[:tall, wide - LANE:wide].astype(F32)
        at = 2 * k
        moved = first if at == 0 else pltpu.roll(first, at, 1)
        packed = jnp.where((lane >= at) & (lane < at + 2), moved, packed)
        at = 16 + 2 * k
        packed = jnp.where(
            (lane >= at) & (lane < at + 2), pltpu.roll(last, at + 2, 1), packed
        )
    strip_out[...] = packed.T[:32]

    pl.semaphore_wait(
        barrier,
        n_rows - 1 + n_cols - 1 + sum(exists.astype(jnp.int32) for exists, _, _ in diagonals),
    )

    def remote(source, target, sems, index, to):
        return pltpu.make_async_remote_copy(
            src_ref=source, dst_ref=target, send_sem=sems[0].at[index], recv_sem=sems[1].at[index],
            device_id=to, device_id_type=MESH,
        )

    halo = (halo_send, halo_recv)
    north = (lax.rem(row + n_rows - 1, n_rows), col)
    south = (lax.rem(row + 1, n_rows), col)
    west = (row, lax.rem(col + n_cols - 1, n_cols))
    east = (row, lax.rem(col + 1, n_cols))
    top, bottom = pl.ds(0, EDGE), pl.ds(tall - EDGE, EDGE)
    south_halo, north_halo = pl.ds(tall, EDGE), pl.ds(tall + EDGE, EDGE)
    body = pl.ds(0, wide)
    moves = [
        (has_n, has_s, [
            remote(pad.at[:, top, body], pad.at[:, south_halo, body], halo, 0, north),
            remote(wet_int.at[top], wet_int.at[south_halo], halo, 1, north)]),
        (has_s, has_n, [
            remote(pad.at[:, bottom, body], pad.at[:, north_halo, body], halo, 2, south),
            remote(wet_int.at[bottom], wet_int.at[north_halo], halo, 3, south)]),
        (has_w, has_e, [remote(strip_out.at[pl.ds(0, 16)], strip_in.at[pl.ds(16, 16)], halo, 4, west)]),
        (has_e, has_w, [remote(strip_out.at[pl.ds(16, 16)], strip_in.at[pl.ds(0, 16)], halo, 5, east)]),
    ]
    for i, (exists, dr, dc) in enumerate(diagonals):
        rows_at = top if dr < 0 else bottom
        cols_at = pl.ds(0, LANE) if dc < 0 else pl.ds(wide - LANE, LANE)
        to = (lax.rem(row + dr + n_rows, n_rows), lax.rem(col + dc + n_cols, n_cols))
        moves.append((exists, diagonals[3 - i][0], [
            remote(pad.at[:, rows_at, cols_at], corner.at[i], halo, 6 + 2 * i, to),
            remote(wet_int.at[rows_at, cols_at], corner_wet.at[i], halo, 7 + 2 * i, to)]))
    for exists, _, copies in moves:
        @pl.when(exists)
        def _(copies=copies):
            for copy in copies:
                copy.start()

    lanes16 = lax.broadcasted_iota(jnp.int32, (2 * GROUP, src), 0) % GROUP
    spec_copies = []
    for g in range(groups):
        mine = spectrum[g * 2 * GROUP:(g + 1) * 2 * GROUP]
        turned = jnp.concatenate([-mine[GROUP:], mine[:GROUP]], axis=0)
        total = None
        for part, value in enumerate((mine, turned)):
            chunks[2 * g + part].wait()
            value = value.astype(BF16).astype(F32)
            if src % LANE == 0:
                left = jnp.concatenate(
                    [jnp.where(lanes16 == j, value, 0.0) for j in range(GROUP)], axis=1
                ).astype(BF16)
                right = kern[part, pl.ds(g * GROUP, GROUP)].reshape(GROUP * src, obs)
                term = jnp.dot(left, right, preferred_element_type=F32)
                total = term if total is None else total + term
            else:
                for j in range(GROUP):
                    term = jnp.dot(
                        jnp.where(lanes16 == j, value, 0.0).astype(BF16),
                        kern[part, g * GROUP + j], preferred_element_type=F32,
                    )
                    total = term if total is None else total + term
        for d in range(n_cols):
            spec_out[d, g] = total[:, d * points:(d + 1) * points]
        for k in range(1, n_cols):
            to = lax.rem(col + k, n_cols)
            copy = remote(
                spec_out.at[to, g], spec_in.at[k - 1, g], (spec_send.at[g], spec_recv.at[g]),
                k - 1, (row, to),
            )
            copy.start()
            spec_copies.append(copy)

    for i, (_, arrives, copies) in enumerate(moves):
        @pl.when(arrives)
        def _(copies=copies):
            for copy in copies:
                copy.wait_recv()

        @pl.when(jnp.logical_not(arrives))
        def _(i=i):
            if i == 0:
                pad[:, south_halo, body] = jnp.zeros((4, EDGE, wide), F32)
                wet_int[south_halo] = jnp.zeros((EDGE, wide), jnp.int32)
            elif i == 1:
                pad[:, north_halo, body] = jnp.zeros((4, EDGE, wide), F32)
                wet_int[north_halo] = jnp.zeros((EDGE, wide), jnp.int32)
            elif i == 2:
                strip_in[pl.ds(16, 16)] = jnp.zeros((16, tall), F32)
            elif i == 3:
                strip_in[pl.ds(0, 16)] = jnp.zeros((16, tall), F32)
            else:
                corner[i - 4] = jnp.zeros((4, EDGE, LANE), F32)
                corner_wet[i - 4] = jnp.zeros((EDGE, LANE), jnp.int32)

    beside = jnp.concatenate([strip_in[...], jnp.zeros((LANE - 32, tall), F32)], axis=0).T
    wet_pad[:, :wide] = wet_int[...].astype(F32)
    near = lax.broadcasted_iota(jnp.int32, (EDGE, LANE), 1) < LANE // 2
    for k in range(5):
        side = jnp.where(
            lane < LANE // 2,
            pltpu.roll(beside, LANE - 16 - 2 * k, 1),
            pltpu.roll(beside, LANE - 2 - 2 * k, 1),
        )
        pick = (lambda i: corner[i, k]) if k < 4 else (lambda i: corner_wet[i].astype(F32))
        low = jnp.where(near, pick(0), pick(1))
        high = jnp.where(near, pick(2), pick(3))
        if k < 4:
            pad[k, :tall, wide:] = side
            pad[k, tall:tall + EDGE, wide:] = low
            pad[k, tall + EDGE:, wide:] = high
        else:
            wet_pad[:tall, wide:] = side
            wet_pad[tall:tall + EDGE, wide:] = low
            wet_pad[tall + EDGE:, wide:] = high

    @pl.when(at_edge)
    def _():
        pad[3, tall:tall + 1, :] = jnp.ones((1, wide + LANE), F32)
        wet_pad[tall:tall + 1, :] = jnp.ones((1, wide + LANE), F32)

    def first_step():
        wet, speed_sq = wet_pad[...], pad[3]
        speed = jnp.sqrt(speed_sq)
        face_x, face_y = faces(speed, wet, 1), faces(speed, wet, 0)
        new = step_once(pad[0], pad[1], pad[2], speed_sq, wet, face_x, face_y)
        for k in range(3):
            mid[k] = new[k]

    def second_step():
        wet, speed_sq = wet_pad[...], pad[3]
        speed = jnp.sqrt(speed_sq)
        face_x, face_y = faces(speed, wet, 1), faces(speed, wet, 0)
        new = step_once(mid[0], mid[1], mid[2], speed_sq, wet, face_x, face_y)
        for k in range(3):
            out_buf[k] = new[k][:tall, :wide]

    first_step()

    for copy in spec_copies:
        copy.wait_recv()
    highs, lows = [], []
    for g in range(groups):
        value = spec_out[col, g]
        for k in range(1, n_cols):
            value = value + spec_in[k - 1, g]
        high, low = split(value)
        highs.append(high)
        lows.append(low.astype(BF16))
    inputs[7].wait()
    whole_buf[...] = jnp.dot(
        inv[...], jnp.concatenate(highs + lows + highs, axis=0), preferred_element_type=F32
    )
    whole_copies = []
    for k in range(1, n_rows):
        to = lax.rem(row + k, n_rows)
        copy = remote(
            whole_buf.at[pl.ds(pl.multiple_of(to * own_steps, own_steps), own_steps)],
            whole_in.at[k - 1], (whole_send, whole_recv), k - 1, (to, col),
        )
        copy.start()
        whole_copies.append(copy)

    second_step()
    outs = (surf_out, qx_out, qy_out)
    results = []
    for k in range(3):
        where = pl.ds(0, tall - EDGE)
        results.append(pltpu.make_async_copy(out_buf.at[k, where], outs[k].at[where], out_sem.at[k]))
        results[-1].start()
    inputs[8].wait()

    for copy in whole_copies:
        copy.wait_recv()
    value = whole_buf[pl.ds(pl.multiple_of(row * own_steps, own_steps), own_steps)]
    for k in range(1, n_rows):
        value = value + whole_in[k - 1]
    series_buf[...] = value
    results.append(pltpu.make_async_copy(series_buf, series_hbm, out_sem.at[3]))
    results[-1].start()

    late_copies = [
        remote(
            series_buf.at[pl.ds(own_steps - EDGE, EDGE)], late_in.at[col], (late_send, late_recv),
            k - 1, (row, lax.rem(col + k, n_cols)),
        )
        for k in range(1, n_cols)
    ]

    @pl.when(at_edge)
    def _():
        for copy in late_copies:
            copy.start()
        span = wide + LANE
        place = lax.broadcasted_iota(jnp.int32, (span, obs), 0)
        place = jnp.where(place >= wide + LANE // 2, place - span, place) + col * wide
        chosen = jnp.where(place == cells[...], 1.0, 0.0).astype(BF16)
        late_in[col] = value[own_steps - EDGE:]
        for k in range(1, n_cols):
            come = lax.rem(col + n_cols - k, n_cols)
            remote(
                series_buf.at[pl.ds(own_steps - EDGE, EDGE)], late_in.at[come],
                (late_send, late_recv), k - 1, (row, lax.rem(col + k, n_cols)),
            ).wait_recv()
        latest = jnp.concatenate([late_in[d] for d in range(n_cols)], axis=1)
        high, rest = split(latest)
        middle, rest = split(rest)
        parts = jnp.concatenate([high.astype(F32), middle.astype(F32), rest, rest], axis=0)
        picked = lax.dot_general(
            parts.astype(BF16), chosen, (((1,), (1,)), ((), ())), preferred_element_type=F32
        )
        picked = picked[:EDGE] + picked[EDGE:2 * EDGE] + picked[2 * EDGE:3 * EDGE]
        base = tall - 2 * EDGE
        part_rows = pl.ds(base, 3 * EDGE)
        at_ghost = lax.broadcasted_iota(jnp.int32, (3 * EDGE, span), 0) == 2 * EDGE
        ghosts = [
            jnp.broadcast_to(picked[EDGE - 2 + k:EDGE - 1 + k], (3 * EDGE, span)) for k in range(2)
        ]
        wet, speed_sq = wet_pad[part_rows], pad[3, part_rows]
        speed = jnp.sqrt(speed_sq)
        face_x, face_y = faces(speed, wet, 1), faces(speed, wet, 0)
        surf = jnp.where(at_ghost, ghosts[0], pad[0, part_rows])
        surf, qx, qy = step_once(
            surf, pad[1, part_rows], pad[2, part_rows], speed_sq, wet, face_x, face_y
        )
        surf = jnp.where(at_ghost, ghosts[1], surf)
        qx = jnp.where(at_ghost, 0.0, qx)
        qy = jnp.where(at_ghost, 0.0, qy)
        new = step_once(surf, qx, qy, speed_sq, wet, face_x, face_y)
        for k in range(3):
            out_buf[k, tall - EDGE:] = new[k][EDGE:2 * EDGE, :wide]

    for k in range(3):
        where = pl.ds(tall - EDGE, EDGE)
        results.append(
            pltpu.make_async_copy(out_buf.at[k, where], outs[k].at[where], out_sem.at[4 + k])
        )
        results[-1].start()
    for exists, _, copies in moves:
        @pl.when(exists)
        def _(copies=copies):
            for copy in copies:
                copy.wait_send()
    for copy in spec_copies + whole_copies:
        copy.wait_send()

    @pl.when(at_edge)
    def _():
        for copy in late_copies:
            copy.wait_send()

    for copy in results:
        copy.wait()


def on_device(n_rows, n_cols, kernel_hat, coefficients, wave_speed_sq, wet_mask, boundary_cell, height, flux_x, flux_y):
    _, freqs, src, obs = kernel_hat.shape
    steps = coefficients.shape[0]
    tall, wide = height.shape
    groups = freqs // GROUP
    points = obs // n_cols
    own_steps = steps // n_rows
    span = wide + LANE
    forward, inverse = tables(freqs * n_rows, steps, n_rows)
    dma = pltpu.SemaphoreType.DMA
    anywhere = pl.BlockSpec(memory_space=pl.ANY)
    return pl.pallas_call(
        functools.partial(kernel, n_rows, n_cols),
        out_shape=(
            jax.ShapeDtypeStruct((own_steps, points), F32),
            jax.ShapeDtypeStruct((tall, wide), F32),
            jax.ShapeDtypeStruct((tall, wide), F32),
            jax.ShapeDtypeStruct((tall, wide), F32),
        ),
        in_specs=[anywhere] * 10,
        out_specs=(anywhere,) * 4,
        scratch_shapes=[
            pltpu.VMEM(kernel_hat.shape, BF16),
            pltpu.VMEM(coefficients.shape, F32),
            pltpu.VMEM(forward.shape[1:], F32),
            pltpu.VMEM(inverse.shape[1:], BF16),
            pltpu.VMEM((1, obs), jnp.int32),
            pltpu.VMEM((4, tall + 2 * EDGE, span), F32),
            pltpu.VMEM((tall + 2 * EDGE, wide), jnp.int32),
            pltpu.VMEM((tall + 2 * EDGE, span), F32),
            pltpu.VMEM((4, 4, EDGE, LANE), F32),
            pltpu.VMEM((4, EDGE, LANE), jnp.int32),
            pltpu.VMEM((32, tall), F32),
            pltpu.VMEM((32, tall), F32),
            pltpu.VMEM((n_cols, groups, 2 * GROUP, points), F32),
            pltpu.VMEM((n_cols - 1, groups, 2 * GROUP, points), F32),
            pltpu.VMEM((steps, points), F32),
            pltpu.VMEM((n_rows - 1, own_steps, points), F32),
            pltpu.VMEM((own_steps, points), F32),
            pltpu.VMEM((n_cols, EDGE, points), F32),
            pltpu.VMEM((3, tall + 2 * EDGE, span), F32),
            pltpu.VMEM((3, tall, wide), F32),
            dma((9,)),
            dma((groups, 2)),
            dma((14,)),
            dma((14,)),
            dma((groups, n_cols - 1)),
            dma((groups, n_cols - 1)),
            dma((n_rows - 1,)),
            dma((n_rows - 1,)),
            dma((n_cols - 1,)),
            dma((n_cols - 1,)),
            dma((7,)),
        ],
        compiler_params=pltpu.CompilerParams(
            collective_id=0, has_side_effects=True, vmem_limit_bytes=60 * 1024 * 1024
        ),
    )(
        kernel_hat, coefficients, wave_speed_sq, wet_mask, boundary_cell.reshape(1, obs),
        height, flux_x, flux_y, jnp.asarray(forward), jnp.asarray(inverse),
    )


def solution(mesh):
    n_rows, n_cols = mesh.shape["rows"], mesh.shape["cols"]
    return jax.shard_map(
        functools.partial(on_device, n_rows, n_cols),
        mesh=mesh,
        in_specs=(
            P(None, "rows", "cols", None),
            P(None, "cols"),
            P("rows", "cols"),
            P("rows", "cols"),
            P(),
            P("rows", "cols"),
            P("rows", "cols"),
            P("rows", "cols"),
        ),
        out_specs=(P("rows", "cols"), P("rows", "cols"), P("rows", "cols"), P("rows", "cols")),
        check_vma=False,
    )
```

time: 185 us -> 28.3 us (0.15)
  waiting for transfers between devices: 69.1 us -> 0 us
  starting transfers between devices: 57.2 us -> 0 us
  Pallas kernels: 0 us -> 21.1 us
  other arithmetic: 16.3 us -> 0 us
  matrix products: 16.1 us -> 0 us
  between operations: 14.8 us -> 0.64 us
  blocking collectives: 5.18 us -> 0 us
    reduce_scatter x2 -> x0, waiting for transfers between devices: 66.6 us -> none  [the longest x1 66.6 us: on_device(): lax.psum_scatter(partial_value, 'rows', scatter_dimension=0, tiled=True)]
    ppermute x20 -> x0, starting transfers between devices: 57.1 us -> none  [the longest x10 44.2 us: with_halo(): lax.ppermute(tail, axis, [(i, (i + 1) % count) for i in range(ends)])]
    pallas_call x0 -> x1, Pallas kernels: none -> 21.1 us  [on_device(): pl.pallas_call(functools.partial(kernel, n_rows, n_cols), out_shape=(jax....]
    dot_general x9 -> x0, matrix products: 16.1 us -> none  [the longest x1 5.33 us: on_device(): jnp.einsum(form, kern_im, coef_re, preferred_element_type=jnp.float32)]
    mul x10 -> x0, other arithmetic: 14 us -> none  [the longest x4 5.57 us: face_fluxes(): opened * (0.5 * (left_sq * left_surf + right_sq * right_surf) - damping *...]
    all_gather x1 -> x0, blocking collectives: 5.18 us -> none  [on_device(): latest = lax.all_gather(series[-2:], 'cols', axis=1, tiled=True)]
    unnamed x22 -> x4, local copies, waits for them, and re-layouts: 1.19 us -> 6.33 us
    ppermute x20 -> x0, waiting for transfers between devices: 2.52 us -> none  [the longest x10 2.5 us: with_halo(): lax.ppermute(head, axis, [((i + 1) % count, i) for i in range(ends)])]
  transfers between devices with their start and end apart: 22 -> 0, of which waited for: 2 -> 0; matrix products, arithmetic and copies ran while one was open for 11% -> 0% of each run, Pallas kernels for 0% -> 0%
where the time goes in v1:
time: 28.3 us; the launch traced here: 28.1 us
  Pallas kernels  21.1 us (75%)
  local copies, waits for them, and re-layouts  6.33 us (22%)
  between operations  0.64 us (2%)
    pallas_call x1, Pallas kernels, on_device(): pl.pallas_call(functools.partial(kernel, n_rows, n_cols), out_shape=(jax....  21.1 us
    unnamed x4, local copies, waits for them, and re-layouts  6.33 us

profile of v1, /device:TPU:0, one launch (start us, length us, event | category | flops | bytes accessed | tf_op | source)
XLA Modules:
  0.0 28.1 jit_solution(13206165570352288752)
XLA Ops:
  0.6 21.1 %shard_map.129 = (f32[16,256]{1,0:T(8,128)}, f32[256,256]{1,0:T(8,128)}, f32[256,256]{1,0:T(8,128)}, f32[256,256]{1,0:T(8,128)}) custom-call(bf16[2,32,128,1024]{3,2,1,0:T(8,128)(2,1)} %kern_hbm.1, f32[128,128]{1,0:T(8,128)} %coef_hbm.1, f32[256,256]{1,0:T(8,128)} %sq_hbm.1, s32[256,256]{1,0:T(8,128)} %wet_hbm.1, s32[1,1024]{1,0:T(1,128)} %bitcast.1, ...), custom_call_target="tpu_custom_call" | custom-call | tf_op jit(solution)/shard_map/pallas_call | solution.py:415
  21.8 1.3 %copy.18 = f32[16,256]{1,0:T(8,128)} copy(f32[16,256]{1,0:T(8,128)} %get-tuple-element.8) | data formatting | bytes 32768
  23.1 1.7 %copy.19 = f32[256,256]{1,0:T(8,128)} copy(f32[256,256]{1,0:T(8,128)} %get-tuple-element.9) | data formatting | bytes 524288
  24.7 1.7 %copy.20 = f32[256,256]{1,0:T(8,128)} copy(f32[256,256]{1,0:T(8,128)} %get-tuple-element.10) | data formatting | bytes 524288
  26.4 1.7 %copy.21 = f32[256,256]{1,0:T(8,128)} copy(f32[256,256]{1,0:T(8,128)} %get-tuple-element.11) | data formatting | bytes 524288

commit v2 on v1

--- a/solution.py
+++ b/solution.py
@@ -63,12 +63,12 @@
 def kernel(
     n_rows, n_cols,
     kern_hbm, coef_hbm, sq_hbm, wet_hbm, cell_hbm, surf_hbm, qx_hbm, qy_hbm, fwd_hbm, inv_hbm,
-    series_hbm, surf_out, qx_out, qy_out,
+    series_buf, out_buf,
     kern, coef, fwd, inv, cells, pad, wet_int, wet_pad, corner, corner_wet,
-    strip_out, strip_in, spec_out, spec_in, whole_buf, whole_in, series_buf, late_in,
-    mid, out_buf,
+    strip_out, strip_in, spec_out, spec_in, whole_buf, whole_in, late_in,
+    mid,
     local_sem, kern_sem, halo_send, halo_recv, spec_send, spec_recv,
-    whole_send, whole_recv, late_send, late_recv, out_sem,
+    whole_send, whole_recv, late_send, late_recv,
 ):
     row = lax.axis_index("rows")
     col = lax.axis_index("cols")
@@ -310,12 +310,6 @@
         whole_copies.append(copy)
 
     second_step()
-    outs = (surf_out, qx_out, qy_out)
-    results = []
-    for k in range(3):
-        where = pl.ds(0, tall - EDGE)
-        results.append(pltpu.make_async_copy(out_buf.at[k, where], outs[k].at[where], out_sem.at[k]))
-        results[-1].start()
     inputs[8].wait()
 
     for copy in whole_copies:
@@ -324,8 +318,6 @@
     for k in range(1, n_rows):
         value = value + whole_in[k - 1]
     series_buf[...] = value
-    results.append(pltpu.make_async_copy(series_buf, series_hbm, out_sem.at[3]))
-    results[-1].start()
 
     late_copies = [
         remote(
@@ -378,12 +370,6 @@
         for k in range(3):
             out_buf[k, tall - EDGE:] = new[k][EDGE:2 * EDGE, :wide]
 
-    for k in range(3):
-        where = pl.ds(tall - EDGE, EDGE)
-        results.append(
-            pltpu.make_async_copy(out_buf.at[k, where], outs[k].at[where], out_sem.at[4 + k])
-        )
-        results[-1].start()
     for exists, _, copies in moves:
         @pl.when(exists)
         def _(copies=copies):
@@ -397,7 +383,14 @@
         for copy in late_copies:
             copy.wait_send()
 
-    for copy in results:
+
+def write_out(series, fields, series_hbm, surf_hbm, qx_hbm, qy_hbm, sems):
+    copies = [pltpu.make_async_copy(series, series_hbm, sems.at[3])]
+    for k, target in enumerate((surf_hbm, qx_hbm, qy_hbm)):
+        copies.append(pltpu.make_async_copy(fields.at[k], target, sems.at[k]))
+    for copy in copies:
+        copy.start()
+    for copy in copies:
         copy.wait()
 
 
@@ -411,17 +404,16 @@
     span = wide + LANE
     forward, inverse = tables(freqs * n_rows, steps, n_rows)
     dma = pltpu.SemaphoreType.DMA
-    anywhere = pl.BlockSpec(memory_space=pl.ANY)
-    return pl.pallas_call(
+    anywhere = pl.BlockSpec(memory_space=pltpu.HBM)
+    in_vmem = pl.BlockSpec(memory_space=pltpu.VMEM)
+    series, fields = pl.pallas_call(
         functools.partial(kernel, n_rows, n_cols),
         out_shape=(
-            jax.ShapeDtypeStruct((own_steps, points), F32),
-            jax.ShapeDtypeStruct((tall, wide), F32),
-            jax.ShapeDtypeStruct((tall, wide), F32),
-            jax.ShapeDtypeStruct((tall, wide), F32),
+            pltpu.VMEM((own_steps, points), F32),
+            pltpu.VMEM((3, tall, wide), F32),
         ),
         in_specs=[anywhere] * 10,
-        out_specs=(anywhere,) * 4,
+        out_specs=(in_vmem,) * 2,
         scratch_shapes=[
             pltpu.VMEM(kernel_hat.shape, BF16),
             pltpu.VMEM(coefficients.shape, F32),
@@ -439,10 +431,8 @@
             pltpu.VMEM((n_cols - 1, groups, 2 * GROUP, points), F32),
             pltpu.VMEM((steps, points), F32),
             pltpu.VMEM((n_rows - 1, own_steps, points), F32),
-            pltpu.VMEM((own_steps, points), F32),
             pltpu.VMEM((n_cols, EDGE, points), F32),
             pltpu.VMEM((3, tall + 2 * EDGE, span), F32),
-            pltpu.VMEM((3, tall, wide), F32),
             dma((9,)),
             dma((groups, 2)),
             dma((14,)),
@@ -453,7 +443,6 @@
             dma((n_rows - 1,)),
             dma((n_cols - 1,)),
             dma((n_cols - 1,)),
-            dma((7,)),
         ],
         compiler_params=pltpu.CompilerParams(
             collective_id=0, has_side_effects=True, vmem_limit_bytes=60 * 1024 * 1024
@@ -462,6 +451,19 @@
         kernel_hat, coefficients, wave_speed_sq, wet_mask, boundary_cell.reshape(1, obs),
         height, flux_x, flux_y, jnp.asarray(forward), jnp.asarray(inverse),
     )
+    return pl.pallas_call(
+        write_out,
+        out_shape=(
+            jax.ShapeDtypeStruct((own_steps, points), F32),
+            jax.ShapeDtypeStruct((tall, wide), F32),
+            jax.ShapeDtypeStruct((tall, wide), F32),
+            jax.ShapeDtypeStruct((tall, wide), F32),
+        ),
+        in_specs=[in_vmem] * 2,
+        out_specs=(anywhere,) * 4,
+        scratch_shapes=[dma((4,))],
+        compiler_params=pltpu.CompilerParams(vmem_limit_bytes=4 * 1024 * 1024),
+    )(series, fields)
 
 
 def solution(mesh):

time: 28.3 us -> 22.2 us (0.78)
  local copies, waits for them, and re-layouts: 6.33 us -> 0 us
  Pallas kernels: 21.1 us -> 21.4 us
    unnamed x4 -> x0, local copies, waits for them, and re-layouts: 6.33 us -> none
    pallas_call x1 -> x2, Pallas kernels: 21.1 us -> 21.4 us  [the longest x1 20.5 us: on_device(): pl.pallas_call(functools.partial(kernel, n_rows, n_cols), out_shape=(pltp...]
where the time goes in v2:
time: 22.2 us; the launch traced here: 22 us
  Pallas kernels  21.4 us (96%)
  between operations  0.64 us (3%)
    pallas_call x1, Pallas kernels, on_device(): pl.pallas_call(functools.partial(kernel, n_rows, n_cols), out_shape=(pltp...  20.5 us
    pallas_call x1, Pallas kernels, on_device(): pl.pallas_call(write_out, out_shape=(jax.ShapeDtypeStruct((own_steps, poi...  0.92 us

profile of v2, /device:TPU:0, one launch (start us, length us, event | category | flops | bytes accessed | tf_op | source)
XLA Modules:
  0.0 22.0 jit_solution(6468059919163878435)
XLA Ops:
  0.6 20.5 %shard_map.129 = (f32[16,256]{1,0:T(8,128)S(1)}, f32[3,256,256]{2,1,0:T(8,128)S(1)}) custom-call(bf16[2,32,128,1024]{3,2,1,0:T(8,128)(2,1)} %kern_hbm.1, f32[128,128]{1,0:T(8,128)} %coef_hbm.1, f32[256,256]{1,0:T(8,128)} %sq_hbm.1, s32[256,256]{1,0:T(8,128)} %wet_hbm.1, s32[1,1024]{1,0:T(1,128)} %bitcast.1, f32[256,256]{1,0:T(8,128)} %surf_hbm.1, ...), custom_call_target="tpu_custom_call" | custom-call | tf_op jit(solution)/shard_map/pallas_call | solution.py:409
  21.1 0.9 %shard_map.130 = (f32[16,256]{1,0:T(8,128)}, f32[256,256]{1,0:T(8,128)}, f32[256,256]{1,0:T(8,128)}, f32[256,256]{1,0:T(8,128)}) custom-call(f32[16,256]{1,0:T(8,128)S(1)} %get-tuple-element.6.series, f32[3,256,256]{2,1,0:T(8,128)S(1)} %get-tuple-element.7.fields), custom_call_target="tpu_custom_call" | custom-call | tf_op jit(solution)/shard_map/pallas_call | solution.py:454

commit v3 on v2

--- a/solution.py
+++ b/solution.py
@@ -65,8 +65,8 @@
     kern_hbm, coef_hbm, sq_hbm, wet_hbm, cell_hbm, surf_hbm, qx_hbm, qy_hbm, fwd_hbm, inv_hbm,
     series_buf, out_buf,
     kern, coef, fwd, inv, cells, pad, wet_int, wet_pad, corner, corner_wet,
-    strip_out, strip_in, spec_out, spec_in, whole_buf, whole_in, late_in,
-    mid,
+    strip_out, strip_in, spec_out, spec_in, whole_buf, whole_in, late_out, late_in, latest_buf,
+    mid, chosen_buf,
     local_sem, kern_sem, halo_send, halo_recv, spec_send, spec_recv,
     whole_send, whole_recv, late_send, late_recv,
 ):
@@ -113,6 +113,17 @@
         pl.semaphore_signal(barrier, 1, device_id=(lax.rem(row + k, n_rows), col), device_id_type=MESH)
     for k in range(1, n_cols):
         pl.semaphore_signal(barrier, 1, device_id=(row, lax.rem(col + k, n_cols)), device_id_type=MESH)
+    for k in range(1, n_cols):
+        other = lax.rem(col + k, n_cols)
+
+        @pl.when(jnp.logical_not(at_edge))
+        def _(other=other):
+            pl.semaphore_signal(barrier, 1, device_id=(n_rows - 1, other), device_id_type=MESH)
+
+        @pl.when(at_edge)
+        def _(other=other):
+            for r in range(n_rows - 1):
+                pl.semaphore_signal(barrier, 1, device_id=(r, other), device_id_type=MESH)
     for exists, dr, dc in diagonals:
         @pl.when(exists)
         def _(dr=dr, dc=dc):
@@ -145,7 +156,9 @@
 
     pl.semaphore_wait(
         barrier,
-        n_rows - 1 + n_cols - 1 + sum(exists.astype(jnp.int32) for exists, _, _ in diagonals),
+        n_rows - 1 + n_cols - 1
+        + (n_cols - 1) * jnp.where(at_edge, n_rows - 1, 1)
+        + sum(exists.astype(jnp.int32) for exists, _, _ in diagonals),
     )
 
     def remote(source, target, sems, index, to):
@@ -191,8 +204,9 @@
         mine = spectrum[g * 2 * GROUP:(g + 1) * 2 * GROUP]
         turned = jnp.concatenate([-mine[GROUP:], mine[:GROUP]], axis=0)
         total = None
+        chunks[2 * g].wait()
+        chunks[2 * g + 1].wait()
         for part, value in enumerate((mine, turned)):
-            chunks[2 * g + part].wait()
             value = value.astype(BF16).astype(F32)
             if src % LANE == 0:
                 left = jnp.concatenate(
@@ -296,9 +310,20 @@
         highs.append(high)
         lows.append(low.astype(BF16))
     inputs[7].wait()
-    whole_buf[...] = jnp.dot(
+    whole = jnp.dot(
         inv[...], jnp.concatenate(highs + lows + highs, axis=0), preferred_element_type=F32
     )
+    late_out[...] = whole[whole.shape[0] - 2:]
+    whole_buf[...] = whole
+    late_copies = []
+    for k in range(1, n_cols):
+        copy = pltpu.make_async_remote_copy(
+            src_ref=late_out, dst_ref=late_in.at[k - 1, row],
+            send_sem=late_send.at[k - 1], recv_sem=late_recv.at[k - 1, row],
+            device_id=(n_rows - 1, lax.rem(col + k, n_cols)), device_id_type=MESH,
+        )
+        copy.start()
+        late_copies.append(copy)
     whole_copies = []
     for k in range(1, n_rows):
         to = lax.rem(row + k, n_rows)
@@ -311,6 +336,13 @@
 
     second_step()
     inputs[8].wait()
+    span = wide + LANE
+
+    @pl.when(at_edge)
+    def _():
+        place = lax.broadcasted_iota(jnp.int32, (span, obs), 0)
+        place = jnp.where(place >= wide + LANE // 2, place - span, place) + col * wide
+        chosen_buf[...] = jnp.where(place == cells[...], 1.0, 0.0).astype(BF16)
 
     for copy in whole_copies:
         copy.wait_recv()
@@ -319,42 +351,33 @@
         value = value + whole_in[k - 1]
     series_buf[...] = value
 
-    late_copies = [
-        remote(
-            series_buf.at[pl.ds(own_steps - EDGE, EDGE)], late_in.at[col], (late_send, late_recv),
-            k - 1, (row, lax.rem(col + k, n_cols)),
-        )
-        for k in range(1, n_cols)
-    ]
-
     @pl.when(at_edge)
     def _():
-        for copy in late_copies:
-            copy.start()
-        span = wide + LANE
-        place = lax.broadcasted_iota(jnp.int32, (span, obs), 0)
-        place = jnp.where(place >= wide + LANE // 2, place - span, place) + col * wide
-        chosen = jnp.where(place == cells[...], 1.0, 0.0).astype(BF16)
-        late_in[col] = value[own_steps - EDGE:]
+        latest_buf[col] = value[own_steps - 2:]
         for k in range(1, n_cols):
-            come = lax.rem(col + n_cols - k, n_cols)
-            remote(
-                series_buf.at[pl.ds(own_steps - EDGE, EDGE)], late_in.at[come],
-                (late_send, late_recv), k - 1, (row, lax.rem(col + k, n_cols)),
-            ).wait_recv()
-        latest = jnp.concatenate([late_in[d] for d in range(n_cols)], axis=1)
+            share = None
+            for r in range(n_rows):
+                pltpu.make_async_remote_copy(
+                    src_ref=late_out, dst_ref=late_in.at[k - 1, r],
+                    send_sem=late_send.at[k - 1], recv_sem=late_recv.at[k - 1, r],
+                    device_id=(row, lax.rem(col + k, n_cols)), device_id_type=MESH,
+                ).wait_recv()
+                share = late_in[k - 1, r] if share is None else share + late_in[k - 1, r]
+            latest_buf[lax.rem(col + n_cols - k, n_cols)] = share
+        latest = jnp.concatenate([latest_buf[d] for d in range(n_cols)], axis=1)
         high, rest = split(latest)
         middle, rest = split(rest)
         parts = jnp.concatenate([high.astype(F32), middle.astype(F32), rest, rest], axis=0)
         picked = lax.dot_general(
-            parts.astype(BF16), chosen, (((1,), (1,)), ((), ())), preferred_element_type=F32
-        )
-        picked = picked[:EDGE] + picked[EDGE:2 * EDGE] + picked[2 * EDGE:3 * EDGE]
+            parts.astype(BF16), chosen_buf[...], (((1,), (1,)), ((), ())),
+            preferred_element_type=F32,
+        )
+        picked = picked[0:2] + picked[2:4] + picked[4:6]
         base = tall - 2 * EDGE
         part_rows = pl.ds(base, 3 * EDGE)
         at_ghost = lax.broadcasted_iota(jnp.int32, (3 * EDGE, span), 0) == 2 * EDGE
         ghosts = [
-            jnp.broadcast_to(picked[EDGE - 2 + k:EDGE - 1 + k], (3 * EDGE, span)) for k in range(2)
+            jnp.broadcast_to(picked[k:k + 1], (3 * EDGE, span)) for k in range(2)
         ]
         wet, speed_sq = wet_pad[part_rows], pad[3, part_rows]
         speed = jnp.sqrt(speed_sq)
@@ -375,13 +398,8 @@
         def _(copies=copies):
             for copy in copies:
                 copy.wait_send()
-    for copy in spec_copies + whole_copies:
+    for copy in spec_copies + whole_copies + late_copies:
         copy.wait_send()
-
-    @pl.when(at_edge)
-    def _():
-        for copy in late_copies:
-            copy.wait_send()
 
 
 def write_out(series, fields, series_hbm, surf_hbm, qx_hbm, qy_hbm, sems):
@@ -431,8 +449,11 @@
             pltpu.VMEM((n_cols - 1, groups, 2 * GROUP, points), F32),
             pltpu.VMEM((steps, points), F32),
             pltpu.VMEM((n_rows - 1, own_steps, points), F32),
-            pltpu.VMEM((n_cols, EDGE, points), F32),
+            pltpu.VMEM((2, points), F32),
+            pltpu.VMEM((n_cols - 1, n_rows, 2, points), F32),
+            pltpu.VMEM((n_cols, 2, points), F32),
             pltpu.VMEM((3, tall + 2 * EDGE, span), F32),
+            pltpu.VMEM((span, obs), BF16),
             dma((9,)),
             dma((groups, 2)),
             dma((14,)),
@@ -442,7 +463,7 @@
             dma((n_rows - 1,)),
             dma((n_rows - 1,)),
             dma((n_cols - 1,)),
-            dma((n_cols - 1,)),
+            dma((n_cols - 1, n_rows)),
         ],
         compiler_params=pltpu.CompilerParams(
             collective_id=0, has_side_effects=True, vmem_limit_bytes=60 * 1024 * 1024

time: 22.2 us -> 21.9 us (0.986)
  Pallas kernels: 21.4 us -> 21 us
    pallas_call x1, Pallas kernels: 20.5 us -> 20.1 us  [on_device(): pl.pallas_call(functools.partial(kernel, n_rows, n_cols), out_shape=(pltp...]
where the time goes in v3:
time: 21.9 us; the launch traced here: 21.6 us
  Pallas kernels  21 us (96%)
  between operations  0.64 us (3%)
    pallas_call x1, Pallas kernels, on_device(): pl.pallas_call(functools.partial(kernel, n_rows, n_cols), out_shape=(pltp...  20.1 us
    pallas_call x1, Pallas kernels, on_device(): pl.pallas_call(write_out, out_shape=(jax.ShapeDtypeStruct((own_steps, poi...  0.92 us

profile of v3, /device:TPU:0, one launch (start us, length us, event | category | flops | bytes accessed | tf_op | source)
XLA Modules:
  0.0 21.6 jit_solution(6199183258376128710)
XLA Ops:
  0.6 20.1 %shard_map.129 = (f32[16,256]{1,0:T(8,128)S(1)}, f32[3,256,256]{2,1,0:T(8,128)S(1)}) custom-call(bf16[2,32,128,1024]{3,2,1,0:T(8,128)(2,1)} %kern_hbm.1, f32[128,128]{1,0:T(8,128)} %coef_hbm.1, f32[256,256]{1,0:T(8,128)} %sq_hbm.1, s32[256,256]{1,0:T(8,128)} %wet_hbm.1, s32[1,1024]{1,0:T(1,128)} %bitcast.1, f32[256,256]{1,0:T(8,128)} %surf_hbm.1, ...), custom_call_target="tpu_custom_call" | custom-call | tf_op jit(solution)/shard_map/pallas_call | solution.py:427
  20.7 0.9 %shard_map.130 = (f32[16,256]{1,0:T(8,128)}, f32[256,256]{1,0:T(8,128)}, f32[256,256]{1,0:T(8,128)}, f32[256,256]{1,0:T(8,128)}) custom-call(f32[16,256]{1,0:T(8,128)S(1)} %get-tuple-element.6.series, f32[3,256,256]{2,1,0:T(8,128)S(1)} %get-tuple-element.7.fields), custom_call_target="tpu_custom_call" | custom-call | tf_op jit(solution)/shard_map/pallas_call | solution.py:475

commit v4 on v3

--- a/solution.py
+++ b/solution.py
@@ -153,13 +153,6 @@
             (lane >= at) & (lane < at + 2), pltpu.roll(last, at + 2, 1), packed
         )
     strip_out[...] = packed.T[:32]
-
-    pl.semaphore_wait(
-        barrier,
-        n_rows - 1 + n_cols - 1
-        + (n_cols - 1) * jnp.where(at_edge, n_rows - 1, 1)
-        + sum(exists.astype(jnp.int32) for exists, _, _ in diagonals),
-    )
 
     def remote(source, target, sems, index, to):
         return pltpu.make_async_remote_copy(
@@ -192,14 +185,8 @@
         moves.append((exists, diagonals[3 - i][0], [
             remote(pad.at[:, rows_at, cols_at], corner.at[i], halo, 6 + 2 * i, to),
             remote(wet_int.at[rows_at, cols_at], corner_wet.at[i], halo, 7 + 2 * i, to)]))
-    for exists, _, copies in moves:
-        @pl.when(exists)
-        def _(copies=copies):
-            for copy in copies:
-                copy.start()
-
     lanes16 = lax.broadcasted_iota(jnp.int32, (2 * GROUP, src), 0) % GROUP
-    spec_copies = []
+    spec_copies, ready = [], []
     for g in range(groups):
         mine = spectrum[g * 2 * GROUP:(g + 1) * 2 * GROUP]
         turned = jnp.concatenate([-mine[GROUP:], mine[:GROUP]], axis=0)
@@ -224,14 +211,31 @@
                     total = term if total is None else total + term
         for d in range(n_cols):
             spec_out[d, g] = total[:, d * points:(d + 1) * points]
-        for k in range(1, n_cols):
-            to = lax.rem(col + k, n_cols)
-            copy = remote(
-                spec_out.at[to, g], spec_in.at[k - 1, g], (spec_send.at[g], spec_recv.at[g]),
-                k - 1, (row, to),
+        ready.append(g)
+        if g < groups // 2 - 1:
+            continue
+        if g == max(groups // 2 - 1, 0):
+            pl.semaphore_wait(
+                barrier,
+                n_rows - 1 + n_cols - 1
+                + (n_cols - 1) * jnp.where(at_edge, n_rows - 1, 1)
+                + sum(exists.astype(jnp.int32) for exists, _, _ in diagonals),
             )
-            copy.start()
-            spec_copies.append(copy)
+            for exists, _, copies in moves:
+                @pl.when(exists)
+                def _(copies=copies):
+                    for copy in copies:
+                        copy.start()
+        for sent in ready:
+            for k in range(1, n_cols):
+                to = lax.rem(col + k, n_cols)
+                copy = remote(
+                    spec_out.at[to, sent], spec_in.at[k - 1, sent],
+                    (spec_send.at[sent], spec_recv.at[sent]), k - 1, (row, to),
+                )
+                copy.start()
+                spec_copies.append(copy)
+        ready = []
 
     for i, (_, arrives, copies) in enumerate(moves):
         @pl.when(arrives)

time: 21.9 us -> 23.5 us (1.073)
  Pallas kernels: 21 us -> 22.7 us
    pallas_call x1, Pallas kernels: 20.1 us -> 21.8 us  [on_device(): pl.pallas_call(functools.partial(kernel, n_rows, n_cols), out_shape=(pltp...]
where the time goes in v4:
time: 23.5 us; the launch traced here: 23.3 us
  Pallas kernels  22.7 us (97%)
  between operations  0.64 us (3%)
    pallas_call x1, Pallas kernels, on_device(): pl.pallas_call(functools.partial(kernel, n_rows, n_cols), out_shape=(pltp...  21.8 us
    pallas_call x1, Pallas kernels, on_device(): pl.pallas_call(write_out, out_shape=(jax.ShapeDtypeStruct((own_steps, poi...  0.92 us

profile of v4, /device:TPU:0, one launch (start us, length us, event | category | flops | bytes accessed | tf_op | source)
XLA Modules:
  0.0 23.3 jit_solution(3638594762097905244)
XLA Ops:
  0.6 21.8 %shard_map.129 = (f32[16,256]{1,0:T(8,128)S(1)}, f32[3,256,256]{2,1,0:T(8,128)S(1)}) custom-call(bf16[2,32,128,1024]{3,2,1,0:T(8,128)(2,1)} %kern_hbm.1, f32[128,128]{1,0:T(8,128)} %coef_hbm.1, f32[256,256]{1,0:T(8,128)} %sq_hbm.1, s32[256,256]{1,0:T(8,128)} %wet_hbm.1, s32[1,1024]{1,0:T(1,128)} %bitcast.1, f32[256,256]{1,0:T(8,128)} %surf_hbm.1, ...), custom_call_target="tpu_custom_call" | custom-call | tf_op jit(solution)/shard_map/pallas_call | solution.py:431
  22.4 0.9 %shard_map.130 = (f32[16,256]{1,0:T(8,128)}, f32[256,256]{1,0:T(8,128)}, f32[256,256]{1,0:T(8,128)}, f32[256,256]{1,0:T(8,128)}) custom-call(f32[16,256]{1,0:T(8,128)S(1)} %get-tuple-element.6.series, f32[3,256,256]{2,1,0:T(8,128)S(1)} %get-tuple-element.7.fields), custom_call_target="tpu_custom_call" | custom-call | tf_op jit(solution)/shard_map/pallas_call | solution.py:479
